TPU v7x, 32 devices: a whole 2x2x4 slice. The times are simulated.
32 devices in a mesh: section: 2 (over y), dp: 16 (over z, x, core).
Axes of the slice: x: 2, y: 2, z: 4, core: 2. Of those that a mesh axis runs over, the one named last changes fastest.
Arguments:
- activations: bfloat16 [2, 4, 16, 14336], P('section', None, 'dp'), may hold values from -6 to 6
- out_grads: bfloat16 [2, 4, 16, 4096], P('section', None, 'dp'), may hold values from -6 to 6
- basis_in: bfloat16 [2, 14336, 1024], P('section', 'dp'), may hold values from -0.046875 to 0.046875
- basis_out: bfloat16 [2, 4096, 1024], P('section', 'dp'), may hold values from -0.09375 to 0.09375
- eigen_values: float32 [2, 1024, 1024], P('section', 'dp'), may hold values from 0.02 to 2
- query_proj: bfloat16 [2, 8, 1024, 1024], P('section', None, 'dp'), may hold values from -0.046875 to 0.046875
- lengths: int32 [4], replicated, may hold values from 4 to 16
- seq_rows: int32 [4], replicated, may hold values from 0 to 127
- prior_table: float32 [128, 8], P('dp'), may hold values from -6 to 6
Outputs:
- influence: float32 [2, 128, 8], P('section', 'dp')
All inputs are finite; a program needn't handle non-finite values.
Results may differ from a plain program's by a relative error of at most 0.01.
Values may be sent and summed in bfloat16 or wider, within the bound.
No kernel may reach another device: no remote copies, remote signals or barrier semaphores. Data moves between devices by JAX's collectives and lax.ppermute only.
A program may use at most 64 MiB of HBM per device.

v0:
```python
import jax
import jax.numpy as jnp
from jax import lax
from jax.sharding import PartitionSpec as P

DAMPING = 0.01


def entering(value, axis, join, neutral):
    count, mine = (lax.axis_size(axis), lax.axis_index(axis))
    pieces = lax.all_gather(value, axis)
    running = jnp.full_like(value, 0) + jnp.asarray(neutral, value.dtype)

    def step(position, running):
        longer = join(running, pieces[position])
        return jnp.where(position < mine, longer, running)

    return lax.fori_loop(0, count - 1, step, running)


def add_pair(earlier, latter):
    return earlier + latter


def per_device(
    activations,
    out_grads,
    basis_in,
    basis_out,
    eigen_values,
    query_proj,
    lengths,
    seq_rows,
    prior_table,
):
    micro = activations.shape[1]
    cols_acts, cols_grads = (
        lax.all_to_all(activations[0], "dp", split_axis=2, concat_axis=1, tiled=True),
        lax.all_to_all(out_grads[0], "dp", split_axis=2, concat_axis=1, tiled=True),
    )
    slots = cols_acts.shape[1]
    rank_size = basis_in.shape[2]
    act_part = jnp.dot(
        cols_acts.reshape(micro * slots, cols_acts.shape[2]),
        basis_in[0],
        preferred_element_type=jnp.float32,
    )
    grad_part = jnp.dot(
        cols_grads.reshape(micro * slots, cols_grads.shape[2]),
        basis_out[0],
        preferred_element_type=jnp.float32,
    )
    grad_share = lax.psum_scatter(grad_part, "dp", scatter_dimension=1, tiled=True).astype(
        jnp.bfloat16
    )
    act_proj = lax.psum(act_part, "dp").astype(jnp.bfloat16)
    block_rows = grad_share.shape[1]
    position = jnp.arange(slots, dtype=jnp.int32)
    live_mask = (position[None, :] < lengths[:, None]).reshape(micro * slots, 1)
    grad_share = jnp.where(live_mask, grad_share, jnp.zeros_like(grad_share))
    inverse_len = 1.0 / lengths.astype(jnp.float32)
    seq_block = (
        jnp.einsum(
            "mti,mtj->mij",
            grad_share.reshape(micro, slots, block_rows),
            act_proj.reshape(micro, slots, rank_size),
            preferred_element_type=jnp.float32,
        )
        * inverse_len[:, None, None]
    )
    precond = (query_proj[0].astype(jnp.float32) / (eigen_values[0][None] + DAMPING)).astype(
        jnp.bfloat16
    )
    partial_value = jnp.einsum(
        "mij,qij->mq", seq_block, precond.astype(jnp.float32), precision=lax.Precision.HIGHEST
    )
    table_rows = prior_table.shape[0]
    first_row = lax.axis_index("dp") * table_rows
    summed = lax.psum(partial_value, "dp")
    before = entering(summed, "section", add_pair, jnp.zeros_like(summed))
    owner_mask = (
        seq_rows[None, :] == (first_row + jnp.arange(table_rows, dtype=jnp.int32))[:, None]
    ).astype(jnp.float32)
    result = prior_table + jnp.dot(owner_mask, before + summed, precision=lax.Precision.HIGHEST)
    return result[None]


def solution(mesh):
    return jax.shard_map(
        per_device,
        mesh=mesh,
        in_specs=(
            P("section", None, "dp", None),
            P("section", None, "dp", None),
            P("section", "dp", None),
            P("section", "dp", None),
            P("section", "dp", None),
            P("section", None, "dp", None),
            P(),
            P(),
            P("dp", None),
        ),
        out_specs=P("section", "dp", None),
        check_vma=False,
    )
```

profile of v0, /device:TPU:0, one launch (start us, length us, event | category | flops | bytes accessed | tf_op | source)
XLA Modules:
  0.0 303.3 jit_solution(3628222360008374152)
XLA Ops:
  6.5 0.0 copy-start
  6.5 5.0 %copy.14 = bf16[4,1,4096]{0,1,2:T(2,128)(2,1)} copy(bf16[4,1,4096]{2,0,1:T(4,128)(2,1)} %bitcast.47) | data formatting | bytes 65536 | tf_op jit(solution)/shard_map/squeeze | solution.py:39
  11.5 0.5 broadcast.36
  12.1 0.0 copy-start.7
  12.1 0.0 copy-start.3
  12.1 23.5 %reduce = bf16[4096,4]{1,0:T(8,128)(2,1)S(1)} reduce(bf16[4096,1,4]{2,1,0:T(2,128)(2,1)} %bitcast.42, bf16[]{:T(256)} %broadcast.36), dimensions={1}, to_apply=%bitcast.32.reduce_sub_computation | reduce | bytes 65538
  35.5 2.6 reshape.67
  38.1 7.4 %all-to-all-start = ((bf16[16,2,512]{2,1,0:T(2,128)(2,1)}), bf16[16,2,512]{2,1,0:T(2,128)(2,1)S(1)}, u32[]{:S(2)}, u32[]{:S(2)}) async-start(bf16[16,2,512]{2,1,0:T(2,128)(2,1)} %reshape.67), calls=%async_computation | async-start | bytes 65536 | tf_op jit(solution)/shard_map/all_to_all | solution.py:39
  45.5 0.0 copy-done.7
  45.6 0.1 iota_compare_fusion
  45.6 0.5 convert_divide_fusion.1
  46.2 0.0 copy-done.3
  46.2 11.6 %copy.16 = bf16[4,1,14336]{0,1,2:T(2,128)(2,1)} copy(bf16[4,1,14336]{2,0,1:T(4,128)(2,1)S(1)} %bitcast.45) | data formatting | bytes 229376 | tf_op jit(solution)/shard_map/squeeze | solution.py:38
  57.7 79.8 %reduce.1 = bf16[14336,4]{1,0:T(8,128)(2,1)} reduce(bf16[14336,1,4]{2,1,0:T(2,128)(2,1)} %bitcast.41, bf16[]{:T(256)} %broadcast.36), dimensions={1}, to_apply=%bitcast.34.reduce_sub_computation | reduce | bytes 229378
  137.6 0.0 copy-start.2
  137.6 8.3 %reshape.69 = bf16[16,2,1792]{2,1,0:T(2,128)(2,1)} reshape(bf16[14336,4]{1,0:T(8,128)(2,1)} %reduce.1) | data formatting | bytes 229376
  145.8 0.6 lt.31
  146.4 0.0 copy-done.2
  146.5 1.5 fusion
  148.0 0.5 iota_add_fusion
  148.6 0.0 all-to-all-done
  148.6 6.0 %all-to-all-start.1 = ((bf16[16,2,1792]{2,1,0:T(2,128)(2,1)}), bf16[16,2,1792]{2,1,0:T(2,128)(2,1)S(1)}, u32[]{:S(2)}, u32[]{:S(2)}) async-start(bf16[16,2,1792]{2,1,0:T(2,128)(2,1)} %reshape.69), calls=%async_computation.1 | async-start | bytes 229376 | tf_op jit(solution)/shard_map/all_to_all | solution.py:38
  154.6 0.0 copy-start.1
  154.6 0.0 reduce-scatter.4.cloned.1.call-start
  154.6 4.5 %reshape.68 = bf16[4096,1,4]{2,1,0:T(2,128)(2,1)} reshape(bf16[16,2,512]{2,1,0:T(2,128)(2,1)S(1)} %all-to-all-done) | data formatting | bytes 65536
  159.2 4.5 %copy.15 = bf16[4,1,4096]{2,0,1:T(4,128)(2,1)S(1)} copy(bf16[4,1,4096]{0,1,2:T(2,128)(2,1)} %bitcast.43) | data formatting | bytes 65536 | tf_op jit(solution)/shard_map/all_to_all | solution.py:39
  163.7 0.6 reshape.47
  164.3 0.0 copy-done.1
  164.4 1.9 convolution_bitcast_fusion
  166.2 0.0 reduce-scatter.4.cloned.1.call-update
  166.3 0.0 all-to-all-done.1
  166.3 11.5 %reshape.70 = bf16[14336,1,4]{2,1,0:T(2,128)(2,1)} reshape(bf16[16,2,1792]{2,1,0:T(2,128)(2,1)S(1)} %all-to-all-done.1) | data formatting | bytes 229376
  177.8 13.9 %copy.17 = bf16[4,1,14336]{2,0,1:T(4,128)(2,1)S(1)} copy(bf16[4,1,14336]{0,1,2:T(2,128)(2,1)} %bitcast.40) | data formatting | bytes 229376 | tf_op jit(solution)/shard_map/all_to_all | solution.py:38
  191.7 0.0 copy-start.5
  191.7 0.0 copy-start.4
  191.8 0.1 reshape.49
  191.8 0.0 copy-done
  191.9 0.4 fusion.1
  192.3 0.0 copy-start.6
  192.3 0.0 copy-start.8
  192.3 0.0 copy-start.9
  192.3 64.6 %all-reduce.1 = bf16[64,1024]{1,0:T(8,128)(2,1)S(1)} all-reduce(f32[64,1024]{1,0:T(8,128)S(1)} %fusion.1), channel_id=1, replica_groups=mesh['section'=2,'dp'=16] {'dp'}, use_global_device_ids=true, to_apply=%region_1.0 | all-reduce | flops 65536 | bytes 393216 | tf_op jit(solution)/shard_map/psum | solution.py:56
  256.9 0.0 reduce-scatter.4.cloned.1.call-done
  257.0 0.8 copy.21
  257.8 0.0 copy-done.5
  257.8 0.1 convert_select_fusion
  257.9 0.0 copy-done.4
  257.9 0.3 convolution_multiply_fusion
  258.3 3.5 %convolution_bitcast_fusion.1 = f32[4,8]{1,0:T(4,128)S(1)} fusion(bf16[8,64,1024]{2,1,0:T(8,128)(2,1)S(1)} %fusion, f32[4,64,1024]{2,1,0:T(8,128)S(1)} %convolution_multiply_fusion), kind=kOutput, calls=%fused_computation.8 | convolution fusion | flops 25165824 | bytes 2097280 | tf_op jit(solution)/shard_map/mij,qij->mq/dot_general | solution.py:74
  261.8 29.5 %psum.15 = f32[4,8]{1,0:T(4,128)S(1)} all-reduce(f32[4,8]{1,0:T(4,128)S(1)} %convolution_bitcast_fusion.1), channel_id=1, replica_groups=mesh['section'=2,'dp'=16] {'dp'}, use_global_device_ids=true, to_apply=%region_2.3 | all-reduce | flops 32 | bytes 256 | tf_op jit(solution)/shard_map/psum | solution.py:79
  291.3 4.4 %all-gather.1 = f32[2,4,8]{2,1,0:T(4,128)S(1)} all-gather(f32[1,4,8]{2,1,0:T(4,128)S(1)} %bitcast.49), channel_id=2, replica_groups=mesh['section'=2,'dp'=16] {'section'}, dimensions={0}, use_global_device_ids=true | all-gather | bytes 384 | tf_op jit(solution)/shard_map/all_gather | solution.py:11
  295.6 0.0 copy-done.6
  295.6 0.0 copy-done.8
  295.6 0.0 copy-done.9
  295.6 0.8 fusion.3
  (1 shorter events, 0.0 us)
Async XLA Ops:
  6.5 185.3 %copy-start = (bf16[1,896,1024]{2,1,0:T(8,128)(2,1)S(1)}, bf16[1,896,1024]{2,1,0:T(8,128)(2,1)}, u32[]{:S(2)}) copy-start(bf16[1,896,1024]{2,1,0:T(8,128)(2,1)} %param.11) | copy-start | bytes 5505028
  12.1 33.5 %copy-start.7 = (s32[4]{0:T(128)S(1)}, s32[4]{0:T(128)}, u32[]{:S(2)}) copy-start(s32[4]{0:T(128)} %param.15) | copy-start | bytes 52
  12.1 34.1 %copy-start.3 = (bf16[1,4,1,14336]{3,1,2,0:T(4,128)(2,1)S(1)}, bf16[1,4,1,14336]{3,1,2,0:T(4,128)(2,1)}, u32[]{:S(2)}) copy-start(bf16[1,4,1,14336]{3,1,2,0:T(4,128)(2,1)} %param.9) | copy-start | bytes 344068
  38.1 110.4 %all-to-all-start = ((bf16[16,2,512]{2,1,0:T(2,128)(2,1)}), bf16[16,2,512]{2,1,0:T(2,128)(2,1)S(1)}, u32[]{:S(2)}, u32[]{:S(2)}) async-start(bf16[16,2,512]{2,1,0:T(2,128)(2,1)} %reshape.67), calls=%async_computation | async-start | bytes 65536 | tf_op jit(solution)/shard_map/all_to_all | solution.py:39
  137.6 8.9 %copy-start.2 = (f32[1,64,1024]{2,1,0:T(8,128)S(1)}, f32[1,64,1024]{2,1,0:T(8,128)}, u32[]{:S(2)}) copy-start(f32[1,64,1024]{2,1,0:T(8,128)} %param.13) | copy-start | bytes 786436
  148.6 17.7 %all-to-all-start.1 = ((bf16[16,2,1792]{2,1,0:T(2,128)(2,1)}), bf16[16,2,1792]{2,1,0:T(2,128)(2,1)S(1)}, u32[]{:S(2)}, u32[]{:S(2)}) async-start(bf16[16,2,1792]{2,1,0:T(2,128)(2,1)} %reshape.69), calls=%async_computation.1 | async-start | bytes 229376 | tf_op jit(solution)/shard_map/all_to_all | solution.py:38
  154.6 9.8 %copy-start.1 = (bf16[1,256,1024]{2,1,0:T(8,128)(2,1)S(1)}, bf16[1,256,1024]{2,1,0:T(8,128)(2,1)}, u32[]{:S(2)}) copy-start(bf16[1,256,1024]{2,1,0:T(8,128)(2,1)} %param.12) | copy-start | bytes 1572868
  154.6 102.4 %reduce-scatter.4.cloned.1.call-start = ((), (), s32[]{:S(2)}) async-start(), calls=%async_computation.3 | async-start | bytes 557056
  191.7 66.1 %copy-start.5 = (pred[64]{0:T(512)(128)(4,1)S(1)}, pred[64]{0:T(512)(128)(4,1)}, u32[]{:S(2)}) copy-start(pred[64]{0:T(512)(128)(4,1)} %lt.31) | copy-start | bytes 196
  191.7 66.1 %copy-start.4 = (f32[4]{0:T(128)S(1)}, f32[4]{0:T(128)}, u32[]{:S(2)}) copy-start(f32[4]{0:T(128)} %convert_divide_fusion.1) | copy-start | bytes 52
  192.3 103.3 %copy-start.6 = (f32[8,8]{1,0:T(8,128)S(1)}, f32[8,8]{1,0:T(8,128)}, u32[]{:S(2)}) copy-start(f32[8,8]{1,0:T(8,128)} %param.17) | copy-start | bytes 772
  192.3 103.3 %copy-start.8 = (s32[4]{0:T(128)S(1)}, s32[4]{0:T(128)}, u32[]{:S(2)}) copy-start(s32[4]{0:T(128)} %param.16) | copy-start | bytes 52
  192.3 103.3 %copy-start.9 = (s32[8]{0:T(128)S(1)}, s32[8]{0:T(128)}, u32[]{:S(2)}) copy-start(s32[8]{0:T(128)} %iota_add_fusion) | copy-start | bytes 100
Sparse Core Ops, SparseCore 0:
  166.4 57.5 reduce-scatter.3
where the time goes:
time: 304 us; the launch traced here: 303 us
  other arithmetic  106 us (35%)
  blocking collectives  98.4 us (32%)
  local copies, waits for them, and re-layouts  64.7 us (21%)
  between operations  13.6 us (4%)
  starting transfers between devices  13.4 us (4%)
  matrix products  6.96 us (2%)
    unnamed x2, other arithmetic  103 us
    psum x1, blocking collectives, per_device(): act_proj = lax.psum(act_part, 'dp').astype(jnp.bfloat16)  64.6 us
    psum x1, blocking collectives, per_device(): summed = lax.psum(partial_value, 'dp')  29.5 us
    unnamed x26, local copies, waits for them, and re-layouts  28.3 us
    all_to_all x1, local copies, waits for them, and re-layouts, per_device(): lax.all_to_all(activations[0], 'dp', split_axis=2, concat_axis=1, tiled=T...  13.9 us
    squeeze x1, local copies, waits for them, and re-layouts, per_device(): activations[0]  11.6 us
    all_to_all x1, starting transfers between devices, per_device(): lax.all_to_all(out_grads[0], 'dp', split_axis=2, concat_axis=1, tiled=True)  7.39 us
  transfers between devices with their start and end apart: 3, of which 0 were waited for; matrix products, arithmetic and copies ran while one was open for 46% of the time, Pallas kernels for 0%

commit v1 on v0

--- a/solution.py
+++ b/solution.py
@@ -4,6 +4,11 @@
 from jax.sharding import PartitionSpec as P
 
 DAMPING = 0.01
+
+
+def derive_layers_all(local_values, comm_axis):
+    block_last = jax.lax.all_gather(local_values, comm_axis)
+    return jnp.sum(block_last, 0)
 
 
 def entering(value, axis, join, neutral):
@@ -53,7 +58,7 @@
     grad_share = lax.psum_scatter(grad_part, "dp", scatter_dimension=1, tiled=True).astype(
         jnp.bfloat16
     )
-    act_proj = lax.psum(act_part, "dp").astype(jnp.bfloat16)
+    act_proj = derive_layers_all(act_part, "dp").astype(jnp.bfloat16)
     block_rows = grad_share.shape[1]
     position = jnp.arange(slots, dtype=jnp.int32)
     live_mask = (position[None, :] < lengths[:, None]).reshape(micro * slots, 1)

time: 304 us -> 322 us (1.059)
  waiting for transfers between devices: 0.04 us -> 79.6 us
  blocking collectives: 98.4 us -> 35.5 us
    psum x1 -> x0, blocking collectives: 64.6 us -> none  [per_device(): act_proj = lax.psum(act_part, 'dp').astype(jnp.bfloat16)]
    all_gather x0 -> x1, waiting for transfers between devices: none -> 50.7 us  [derive_layers_all(): block_last = jax.lax.all_gather(local_values, comm_axis)]
    unnamed x2 -> x3, waiting for transfers between devices: 0.04 us -> 29 us
    unnamed x26 -> x20, local copies, waits for them, and re-layouts: 28.3 us -> 28.3 us
  transfers between devices with their start and end apart: 3 -> 4, of which waited for: 0 -> 2; matrix products, arithmetic and copies ran while one was open for 46% -> 43% of each run, Pallas kernels for 0% -> 0%
where the time goes in v1:
time: 322 us; the launch traced here: 321 us
  other arithmetic  108 us (34%)
  waiting for transfers between devices  79.6 us (25%)
  local copies, waits for them, and re-layouts  63.6 us (20%)
  blocking collectives  35.5 us (11%)
  starting transfers between devices  13.7 us (4%)
  between operations  13.6 us (4%)
  matrix products  6.9 us (2%)
    unnamed x2, other arithmetic  103 us
    all_gather x1, waiting for transfers between devices, derive_layers_all(): block_last = jax.lax.all_gather(local_values, comm_axis)  50.7 us
    psum x1, blocking collectives, per_device(): summed = lax.psum(partial_value, 'dp')  31.2 us
    unnamed x3, waiting for transfers between devices  29 us
    unnamed x20, local copies, waits for them, and re-layouts  28.3 us
    all_to_all x1, local copies, waits for them, and re-layouts, per_device(): lax.all_to_all(activations[0], 'dp', split_axis=2, concat_axis=1, tiled=T...  13.9 us
    squeeze x1, local copies, waits for them, and re-layouts, per_device(): activations[0]  11.6 us
    all_to_all x1, starting transfers between devices, per_device(): lax.all_to_all(out_grads[0], 'dp', split_axis=2, concat_axis=1, tiled=True)  7.39 us
  transfers between devices with their start and end apart: 4, of which 2 were waited for; matrix products, arithmetic and copies ran while one was open for 43% of the time, Pallas kernels for 0%

profile of v1, /device:TPU:0, one launch (start us, length us, event | category | flops | bytes accessed | tf_op | source)
XLA Modules:
  0.0 320.5 jit_solution(16474796855578619910)
XLA Ops:
  6.5 0.0 copy-start
  6.5 5.0 %copy.14 = bf16[4,1,4096]{0,1,2:T(2,128)(2,1)} copy(bf16[4,1,4096]{2,0,1:T(4,128)(2,1)} %bitcast.49) | data formatting | bytes 65536 | tf_op jit(solution)/shard_map/squeeze | solution.py:44
  11.5 0.5 broadcast.36
  12.1 0.0 copy-start.3
  12.1 23.5 %reduce = bf16[4096,4]{1,0:T(8,128)(2,1)S(1)} reduce(bf16[4096,1,4]{2,1,0:T(2,128)(2,1)} %bitcast.43, bf16[]{:T(256)} %broadcast.36), dimensions={1}, to_apply=%bitcast.33.reduce_sub_computation | reduce | bytes 65538
  35.5 2.6 reshape.67
  38.1 7.4 %all-to-all-start = ((bf16[16,2,512]{2,1,0:T(2,128)(2,1)}), bf16[16,2,512]{2,1,0:T(2,128)(2,1)S(1)}, u32[]{:S(2)}, u32[]{:S(2)}) async-start(bf16[16,2,512]{2,1,0:T(2,128)(2,1)} %reshape.67), calls=%async_computation | async-start | bytes 65536 | tf_op jit(solution)/shard_map/all_to_all | solution.py:44
  45.5 0.0 copy-done.3
  45.6 11.6 %copy.16 = bf16[4,1,14336]{0,1,2:T(2,128)(2,1)} copy(bf16[4,1,14336]{2,0,1:T(4,128)(2,1)S(1)} %bitcast.47) | data formatting | bytes 229376 | tf_op jit(solution)/shard_map/squeeze | solution.py:43
  57.2 79.8 %reduce.1 = bf16[14336,4]{1,0:T(8,128)(2,1)} reduce(bf16[14336,1,4]{2,1,0:T(2,128)(2,1)} %bitcast.42, bf16[]{:T(256)} %broadcast.36), dimensions={1}, to_apply=%bitcast.35.reduce_sub_computation | reduce | bytes 229378
  137.0 8.2 %reshape.69 = bf16[16,2,1792]{2,1,0:T(2,128)(2,1)} reshape(bf16[14336,4]{1,0:T(8,128)(2,1)} %reduce.1) | data formatting | bytes 229376
  145.3 0.0 all-to-all-done
  145.3 6.0 %all-to-all-start.1 = ((bf16[16,2,1792]{2,1,0:T(2,128)(2,1)}), bf16[16,2,1792]{2,1,0:T(2,128)(2,1)S(1)}, u32[]{:S(2)}, u32[]{:S(2)}) async-start(bf16[16,2,1792]{2,1,0:T(2,128)(2,1)} %reshape.69), calls=%async_computation.1 | async-start | bytes 229376 | tf_op jit(solution)/shard_map/all_to_all | solution.py:43
  151.3 0.0 copy-start.1
  151.3 0.0 reduce-scatter.4.cloned.1.call-start
  151.3 4.5 %reshape.68 = bf16[4096,1,4]{2,1,0:T(2,128)(2,1)} reshape(bf16[16,2,512]{2,1,0:T(2,128)(2,1)S(1)} %all-to-all-done) | data formatting | bytes 65536
  155.9 4.5 %copy.15 = bf16[4,1,4096]{2,0,1:T(4,128)(2,1)S(1)} copy(bf16[4,1,4096]{0,1,2:T(2,128)(2,1)} %bitcast.44) | data formatting | bytes 65536 | tf_op jit(solution)/shard_map/all_to_all | solution.py:44
  160.4 0.0 copy-done.1
  160.4 1.1 convolution_bitcast_fusion
  161.6 0.0 reduce-scatter.4.cloned.1.call-update
  161.6 0.3 all-gather.5.cloned.1.call-start
  161.9 0.0 all-to-all-done.1
  161.9 11.5 %reshape.70 = bf16[14336,1,4]{2,1,0:T(2,128)(2,1)} reshape(bf16[16,2,1792]{2,1,0:T(2,128)(2,1)S(1)} %all-to-all-done.1) | data formatting | bytes 229376
  173.4 13.9 %copy.17 = bf16[4,1,14336]{2,0,1:T(4,128)(2,1)S(1)} copy(bf16[4,1,14336]{0,1,2:T(2,128)(2,1)} %bitcast.41) | data formatting | bytes 229376 | tf_op jit(solution)/shard_map/all_to_all | solution.py:43
  187.3 0.0 copy-start.5
  187.3 0.0 copy-start.2
  187.4 0.1 reshape.49
  187.4 0.0 copy-done
  187.5 1.1 fusion.1
  188.6 0.0 all-gather.5.cloned.1.call-update
  188.6 0.0 copy-done.5
  188.6 0.1 iota_compare_fusion
  188.7 0.1 lt.31
  188.8 0.0 copy-done.2
  188.8 1.6 fusion
  190.4 28.9 %reduce-scatter.4.cloned.1.call-done = f32[64,64]{1,0:T(8,128)} async-done(((f32[1024,64]{1,0:T(8,128)}), f32[64,64]{1,0:T(8,128)}) %reduce-scatter.4.cloned.1.call-update) | async-done | bytes 16400
  219.3 0.8 copy.21
  220.2 0.1 convert_select_fusion
  220.3 50.7 %all-gather.5.cloned.1.call-done = f32[1024,1024]{1,0:T(8,128)} async-done(((f32[64,1024]{1,0:T(8,128)}), f32[1024,1024]{1,0:T(8,128)}) %all-gather.5.cloned.1.call-update) | async-done | bytes 4194320 | tf_op jit(solution)/shard_map/all_gather | solution.py:10
  270.9 2.5 reduce_sum.9
  273.5 0.0 copy-start.4
  273.5 0.0 copy-start.6
  273.5 0.3 convolution_multiply_fusion
  273.8 3.5 %convolution_bitcast_fusion.1 = f32[4,8]{1,0:T(4,128)S(1)} fusion(bf16[8,64,1024]{2,1,0:T(8,128)(2,1)S(1)} %fusion, f32[4,64,1024]{2,1,0:T(8,128)S(1)} %convolution_multiply_fusion), kind=kOutput, calls=%fused_computation.8 | convolution fusion | flops 25165824 | bytes 2097280 | tf_op jit(solution)/shard_map/mij,qij->mq/dot_general | solution.py:79
  277.3 31.2 %psum.7 = f32[4,8]{1,0:T(4,128)S(1)} all-reduce(f32[4,8]{1,0:T(4,128)S(1)} %convolution_bitcast_fusion.1), channel_id=1, replica_groups=mesh['section'=2,'dp'=16] {'dp'}, use_global_device_ids=true, to_apply=%region_2.3 | all-reduce | flops 32 | bytes 256 | tf_op jit(solution)/shard_map/psum | solution.py:84
  308.5 4.4 %all-gather.2 = f32[2,4,8]{2,1,0:T(4,128)S(1)} all-gather(f32[1,4,8]{2,1,0:T(4,128)S(1)} %bitcast.51), channel_id=3, replica_groups=mesh['section'=2,'dp'=16] {'section'}, dimensions={0}, use_global_device_ids=true | all-gather | bytes 384 | tf_op jit(solution)/shard_map/all_gather | solution.py:16
  312.9 0.0 copy-done.4
  312.9 0.0 copy-done.6
  312.9 0.8 fusion.3
  (4 shorter events, 0.1 us)
Async XLA Ops:
  6.5 180.9 %copy-start = (bf16[1,896,1024]{2,1,0:T(8,128)(2,1)S(1)}, bf16[1,896,1024]{2,1,0:T(8,128)(2,1)}, u32[]{:S(2)}) copy-start(bf16[1,896,1024]{2,1,0:T(8,128)(2,1)} %param.11) | copy-start | bytes 5505028
  12.1 33.5 %copy-start.3 = (bf16[1,4,1,14336]{3,1,2,0:T(4,128)(2,1)S(1)}, bf16[1,4,1,14336]{3,1,2,0:T(4,128)(2,1)}, u32[]{:S(2)}) copy-start(bf16[1,4,1,14336]{3,1,2,0:T(4,128)(2,1)} %param.9) | copy-start | bytes 344068
  38.1 107.1 %all-to-all-start = ((bf16[16,2,512]{2,1,0:T(2,128)(2,1)}), bf16[16,2,512]{2,1,0:T(2,128)(2,1)S(1)}, u32[]{:S(2)}, u32[]{:S(2)}) async-start(bf16[16,2,512]{2,1,0:T(2,128)(2,1)} %reshape.67), calls=%async_computation | async-start | bytes 65536 | tf_op jit(solution)/shard_map/all_to_all | solution.py:44
  145.3 16.6 %all-to-all-start.1 = ((bf16[16,2,1792]{2,1,0:T(2,128)(2,1)}), bf16[16,2,1792]{2,1,0:T(2,128)(2,1)S(1)}, u32[]{:S(2)}, u32[]{:S(2)}) async-start(bf16[16,2,1792]{2,1,0:T(2,128)(2,1)} %reshape.69), calls=%async_computation.1 | async-start | bytes 229376 | tf_op jit(solution)/shard_map/all_to_all | solution.py:43
  151.3 9.2 %copy-start.1 = (bf16[1,256,1024]{2,1,0:T(8,128)(2,1)S(1)}, bf16[1,256,1024]{2,1,0:T(8,128)(2,1)}, u32[]{:S(2)}) copy-start(bf16[1,256,1024]{2,1,0:T(8,128)(2,1)} %param.12) | copy-start | bytes 1572868
  151.3 68.1 %reduce-scatter.4.cloned.1.call-start = ((), (), s32[]{:S(2)}) async-start(), calls=%async_computation.4 | async-start | bytes 557056
  161.6 109.3 %all-gather.5.cloned.1.call-start = ((), (), s32[]{:S(2)}) async-start(), calls=%async_computation.3 | async-start | bytes 4456448 | tf_op jit(solution)/shard_map/all_gather | solution.py:10
  187.3 1.3 copy-start.5
  187.3 1.5 copy-start.2
  273.5 39.4 %copy-start.4 = (f32[8,8]{1,0:T(8,128)S(1)}, f32[8,8]{1,0:T(8,128)}, u32[]{:S(2)}) copy-start(f32[8,8]{1,0:T(8,128)} %param.17) | copy-start | bytes 772
  273.5 39.4 %copy-start.6 = (s32[4]{0:T(128)S(1)}, s32[4]{0:T(128)}, u32[]{:S(2)}) copy-start(s32[4]{0:T(128)} %param.16) | copy-start | bytes 52
Sparse Core Ops, SparseCore 0:
  161.7 57.5 reduce-scatter.3
  221.5 49.3 all-gather.4
